TPU v7x, 32 devices: a whole 2x2x4 slice. The times are simulated.
32 devices in a mesh: outer: 2 (over core), dp: 4 (over z), tensor: 4 (over y, x).
Axes of the slice: x: 2, y: 2, z: 4, core: 2. Of those that a mesh axis runs over, the one named last changes fastest.
Arguments:
- attn: bfloat16 [2048, 8192], P(('outer', 'dp'), 'tensor'), may hold values from -6 to 6
- out_weight: bfloat16 [8192, 8192], P(None, 'tensor'), may hold values from -0.0625 to 0.0625
- resid: bfloat16 [2048, 8192], P(('outer', 'dp'), 'tensor'), may hold values from -8 to 8
- norm_gain: bfloat16 [8192], P('tensor'), may hold values from 0.5 to 1.5
- head: bfloat16 [8192], P('tensor'), may hold values from -1 to 1
- lengths: int32 [32], P(('outer', 'dp')), may hold values from 1 to 64
- pairs: int32 [32, 2], P(('outer', 'dp')), may hold values from 0 to 3, as said below
- pair_valid: int32 [32], P(('outer', 'dp')), may hold values from 0 to 1, as said below
- loss_scale: float32 [1], replicated, may hold values from 1024 to 8192
Outputs:
- loss: float32 [1], replicated
- grad_out_proj: float32 [8192, 8192], P(('outer', 'dp'), 'tensor')
- grad_gain: float32 [8192], P('tensor')
- grad_head: float32 [8192], P('tensor')
Inputs may be any that keep to these rules, and one draw needn't show every extreme that they name: `pairs`: in each pair the two numbers differ; the first pair of each replica is valid. `pair_valid`: the first of each replica's 4 entries is 1.
All inputs are finite; a program needn't handle non-finite values.
Results may differ from a plain program's by a relative error of at most 0.003.
Values may be sent and summed in bfloat16 or wider, within the bound.
A program may use at most 128 MiB of HBM per device.

v0:
```python
import jax
import jax.numpy as jnp
from jax import lax
from jax.sharding import PartitionSpec as P


def shards(attn, out_weight, resid, norm_gain, head, lengths, pairs, pair_valid, loss_scale):
    f32 = jnp.float32
    tok_dev = attn.shape[0]
    feats = resid.shape[1]
    tensor = lax.axis_size("tensor")
    width = feats * tensor
    seqs_dev = lengths.shape[0]
    seq_len = tok_dev // seqs_dev
    valid = pair_valid.astype(f32)
    count = lax.psum(jnp.sum(valid), ("outer", "dp"))
    part = lax.dot_general(out_weight, attn, (((1,), (1,)), ((), ())), preferred_element_type=f32)
    part = part.astype(jnp.bfloat16).reshape(tensor, feats, tok_dev)
    part = lax.all_to_all(part, "tensor", split_axis=0, concat_axis=0, tiled=True)
    z = resid.astype(f32).T + jnp.sum(part.astype(f32), axis=0)
    gain = norm_gain.astype(f32)[:, None]
    headv = head.astype(f32)[:, None]
    both = headv * gain
    sums = lax.psum(jnp.stack([jnp.sum(z * z, axis=0), jnp.sum(z * both, axis=0)]), "tensor")
    inv = 1.0 / jnp.sqrt(sums[0] / width + 1e-05)
    score = sums[1] * inv
    position = jnp.arange(tok_dev)
    seq_of = position // seq_len
    within = position % seq_len
    member = (within[:, None] < lengths[None, :]) & (
        seq_of[:, None] == jnp.arange(seqs_dev)[None, :]
    )
    pooling = member.astype(f32) / lengths.astype(f32)[None, :]
    reward = jnp.sum(pooling * score[:, None], axis=0)
    choose = jnp.arange(seqs_dev)[None, :]
    select = (pairs[:, 0:1] == choose).astype(f32) - (pairs[:, 1:2] == choose).astype(f32)
    margin = jnp.sum(select * reward[None, :], axis=1)
    loss_part = jnp.sum(valid * jax.nn.softplus(-margin))
    dmargin = -loss_scale[0] * valid * jax.nn.sigmoid(-margin) / count
    dreward = jnp.sum(dmargin[:, None] * select, axis=0)
    dscore = jnp.sum(pooling * dreward[None, :], axis=1)
    weight = inv * dscore
    dproj = weight[None, :] * both - z * (inv**3 * dscore * sums[1] / width)[None, :]
    dproj = dproj.astype(jnp.bfloat16)
    zsum = jnp.sum(z * weight[None, :], axis=1)
    gathered = lax.all_gather(dproj, "tensor", axis=0, tiled=True)
    exchanged = lax.all_to_all(gathered, ("outer", "dp"), split_axis=0, concat_axis=1, tiled=True)
    grad_out_proj = jnp.dot(
        exchanged,
        lax.all_gather(attn, ("outer", "dp"), axis=0, tiled=True),
        preferred_element_type=f32,
    )
    zsum, loss_sum = lax.psum((zsum, loss_part), ("outer", "dp"))
    loss = (loss_sum / count).reshape(1)
    return (loss, grad_out_proj, zsum * headv[:, 0], zsum * gain[:, 0])


def solution(mesh):
    return jax.shard_map(
        shards,
        mesh=mesh,
        in_specs=(
            P(("outer", "dp"), "tensor"),
            P(None, "tensor"),
            P(("outer", "dp"), "tensor"),
            P("tensor"),
            P("tensor"),
            P(("outer", "dp")),
            P(("outer", "dp"), None),
            P(("outer", "dp")),
            P(),
        ),
        out_specs=(P(), P(("outer", "dp"), "tensor"), P("tensor"), P("tensor")),
        check_vma=False,
    )
```

profile of v0, /device:TPU:0, one launch (start us, length us, event | category | flops | bytes accessed | tf_op | source)
XLA Modules:
  0.0 368.8 jit_solution(16129040595212171715)
XLA Ops:
  7.2 16.7 %convolution_convert_fusion = bf16[8192,256]{1,0:T(8,128)(2,1)} fusion(bf16[8192,2048]{1,0:T(8,128)(2,1)} %param.10, bf16[256,2048]{1,0:T(8,128)(2,1)} %param.9), kind=kOutput, calls=%fused_computation | convolution fusion | flops 8592031744 | bytes 38797312 | tf_op jit(solution)/shard_map/dot_general | solution.py:17
  23.9 0.0 copy-start
  23.9 0.0 copy-start.3
  23.9 0.0 copy-start.5
  23.9 0.0 copy-start.1
  23.9 0.0 copy-start.2
  23.9 5.3 %all-to-all-start = ((bf16[4,2048,256]{2,1,0:T(8,128)(2,1)}), bf16[4,2048,256]{2,1,0:T(8,128)(2,1)}, u32[]{:S(2)}, u32[]{:S(2)}) async-start(bf16[4,2048,256]{2,1,0:T(8,128)(2,1)} %bitcast.31), calls=%async_computation | async-start | bytes 8388608 | tf_op jit(solution)/shard_map/all_to_all | solution.py:19
  29.3 0.0 all-gather.3.cloned.1.call-start
  29.3 0.0 copy-done
  29.3 0.5 copy.15
  29.8 0.0 copy-done.3
  30.5 0.0 copy-done.5
  30.5 0.0 copy-done.1
  30.5 0.0 copy-done.2
  30.6 0.0 copy-start.4
  30.6 47.4 %all-to-all-done = bf16[4,2048,256]{2,1,0:T(8,128)(2,1)} async-done(((bf16[4,2048,256]{2,1,0:T(8,128)(2,1)}), bf16[4,2048,256]{2,1,0:T(8,128)(2,1)}, u32[]{:S(2)}, u32[]{:S(2)}) %all-to-all-start) | async-done | bytes 4194336 | tf_op jit(solution)/shard_map/all_to_all | solution.py:19
  77.9 3.0 convert_reduce_fusion
  80.9 0.5 multiply_reduce_fusion.2
  81.4 8.9 %psum.28 = f32[2,256]{1,0:T(2,128)S(1)} all-reduce(f32[2,256]{1,0:T(2,128)S(1)} %pad_maximum_fusion), channel_id=1, replica_groups=mesh['outer'=2,'dp'=4,'tensor'=4] {'tensor'}, use_global_device_ids=true, to_apply=%region_3.0 | all-reduce | flops 512 | bytes 4096 | tf_op jit(solution)/shard_map/psum | solution.py:24
  90.3 0.2 multiply_reduce_fusion.4
  90.5 0.2 multiply_reduce_fusion.6
  90.7 0.0 copy-done.4
  90.7 0.6 convert_reduce_fusion.1
  91.3 16.2 %psum.30 = f32[]{:T(128)} all-reduce(f32[]{:T(128)} %get-tuple-element.6), channel_id=1, replica_groups=mesh['outer'=2,'dp'=4,'tensor'=4] {'outer','dp'}, use_global_device_ids=true, to_apply=%region_9.10 | all-reduce | flops 1 | bytes 8 | tf_op jit(solution)/shard_map/psum | solution.py:16
  107.5 0.7 fusion.9
  108.2 0.1 multiply_reduce_fusion.5
  108.3 0.1 multiply_reduce_fusion.3
  108.4 1.5 subtract_convert_fusion
  109.9 0.0 all-gather.3.cloned.1.call-update
  109.9 0.0 all-gather.5.cloned.1.call-start
  110.0 0.7 all-gather.5.cloned.1.call-update
  110.7 50.8 %all-gather.3.cloned.1.call-done = bf16[8192,256]{1,0:T(8,128)(2,1)} async-done(((bf16[2048,256]{1,0:T(8,128)(2,1)}), bf16[8192,256]{1,0:T(8,128)(2,1)}) %all-gather.3.cloned.1.call-update) | async-done | bytes 4194320 | tf_op jit(solution)/shard_map/all_gather | solution.py:46
  161.5 4.6 %all-to-all-start.1 = ((bf16[8,1024,256]{2,1,0:T(8,128)(2,1)}), bf16[8,1024,256]{2,1,0:T(8,128)(2,1)}, u32[]{:S(2)}, u32[]{:S(2)}) async-start(bf16[8,1024,256]{2,1,0:T(8,128)(2,1)} %bitcast.30), calls=%async_computation.1 | async-start | bytes 8388608 | tf_op jit(solution)/shard_map/all_to_all | solution.py:47
  166.1 171.7 %all-reduce = (f32[]{:T(128)}, f32[2048]{0:T(1024)S(1)}) all-reduce(f32[]{:T(128)} %get-tuple-element.7, f32[2048]{0:T(1024)S(1)} %get-tuple-element.11), channel_id=1, replica_groups=mesh['outer'=2,'dp'=4,'tensor'=4] {'outer','dp'}, use_global_device_ids=true, to_apply=%region_7.8 | all-reduce | flops 2049 | bytes 16392 | tf_op jit(solution)/shard_map/psum | solution.py:53
  339.1 0.6 convert_multiply_fusion
  339.7 0.0 all-to-all-done.1
  339.7 6.5 %copy.16 = bf16[1024,8,256]{0,2,1:T(8,128)(2,1)} copy(bf16[1024,8,256]{2,0,1:T(8,128)(2,1)} %bitcast.13) | data formatting | bytes 8388608 | tf_op jit(solution)/shard_map/all_to_all | solution.py:47
  346.2 0.0 all-gather.5.cloned.1.call-done
  346.2 14.6 %fusion.11 = f32[1024,2048]{1,0:T(8,128)} fusion(bf16[1024,2048]{0,1:T(8,128)(2,1)} %bitcast.32, bf16[2048,2048]{1,0:T(8,128)(2,1)} %all-gather.5.cloned.1.call-done), kind=kOutput, calls=%fused_computation.44 | convolution fusion | flops 8589934592 | bytes 20971520 | tf_op jit(solution)/shard_map/dot_general | solution.py:48
  (7 shorter events, 0.1 us)
Async XLA Ops:
  23.9 5.4 %copy-start = (bf16[256,2048]{1,0:T(8,128)(2,1)S(1)}, bf16[256,2048]{1,0:T(8,128)(2,1)}, u32[]{:S(2)}) copy-start(bf16[256,2048]{1,0:T(8,128)(2,1)} %param.11) | copy-start | bytes 3145732
  23.9 5.9 %copy-start.3 = (s32[4]{0:T(128)S(1)}, s32[4]{0:T(128)}, u32[]{:S(2)}) copy-start(s32[4]{0:T(128)} %param.14) | copy-start | bytes 52
  23.9 6.6 %copy-start.5 = (s32[4,2]{0,1:T(2,128)S(1)}, s32[4,2]{0,1:T(2,128)}, u32[]{:S(2)}) copy-start(s32[4,2]{0,1:T(2,128)} %param.15) | copy-start | bytes 100
  23.9 6.6 %copy-start.1 = (bf16[2048]{0:T(1024)(128)(2,1)S(1)}, bf16[2048]{0:T(1024)(128)(2,1)}, u32[]{:S(2)}) copy-start(bf16[2048]{0:T(1024)(128)(2,1)} %param.12) | copy-start | bytes 12292
  23.9 6.6 %copy-start.2 = (bf16[2048]{0:T(1024)(128)(2,1)S(1)}, bf16[2048]{0:T(1024)(128)(2,1)}, u32[]{:S(2)}) copy-start(bf16[2048]{0:T(1024)(128)(2,1)} %param.13) | copy-start | bytes 12292
  23.9 54.0 %all-to-all-start = ((bf16[4,2048,256]{2,1,0:T(8,128)(2,1)}), bf16[4,2048,256]{2,1,0:T(8,128)(2,1)}, u32[]{:S(2)}, u32[]{:S(2)}) async-start(bf16[4,2048,256]{2,1,0:T(8,128)(2,1)} %bitcast.31), calls=%async_computation | async-start | bytes 8388608 | tf_op jit(solution)/shard_map/all_to_all | solution.py:19
  29.3 132.2 %all-gather.3.cloned.1.call-start = ((), (), s32[]{:S(2)}) async-start(), calls=%async_computation.2 | async-start | bytes 5242880 | tf_op jit(solution)/shard_map/all_gather | solution.py:46
  30.6 60.2 %copy-start.4 = (s32[4]{0:T(128)S(1)}, s32[4]{0:T(128)}, u32[]{:S(2)}) copy-start(s32[4]{0:T(128)} %param.16) | copy-start | bytes 52
  109.9 236.3 %all-gather.5.cloned.1.call-start = ((), (), s32[]{:S(2)}) async-start(), calls=%async_computation.3 | async-start | bytes 9437184 | tf_op jit(solution)/shard_map/all_gather | solution.py:50
  161.5 178.2 %all-to-all-start.1 = ((bf16[8,1024,256]{2,1,0:T(8,128)(2,1)}), bf16[8,1024,256]{2,1,0:T(8,128)(2,1)}, u32[]{:S(2)}, u32[]{:S(2)}) async-start(bf16[8,1024,256]{2,1,0:T(8,128)(2,1)} %bitcast.30), calls=%async_computation.1 | async-start | bytes 8388608 | tf_op jit(solution)/shard_map/all_to_all | solution.py:47
Sparse Core Ops, SparseCore 0:
  110.0 51.4 all-gather.2
  163.1 160.7 all-gather.4
where the time goes:
time: 369 us
  blocking collectives  197 us (53%)
  waiting for transfers between devices  98.9 us (27%)
  matrix products  31.4 us (9%)
  between operations  17.3 us (5%)
  starting transfers between devices  9.99 us (3%)
  other arithmetic  7.44 us (2%)
  local copies, waits for them, and re-layouts  7.01 us (2%)
    psum x1, blocking collectives, shards(): zsum, loss_sum = lax.psum((zsum, loss_part), ('outer', 'dp'))  172 us
    all_gather x1, waiting for transfers between devices, shards(): gathered = lax.all_gather(dproj, 'tensor', axis=0, tiled=True)  50.8 us
    all_to_all x1, waiting for transfers between devices, shards(): lax.all_to_all(part, 'tensor', split_axis=0, concat_axis=0, tiled=True)  47.4 us
    dot_general x1, matrix products, shards(): lax.dot_general(out_weight, attn, (((1,), (1,)), ((), ())), preferred_ele...  16.7 us
    psum x1, blocking collectives, shards(): count = lax.psum(jnp.sum(valid), ('outer', 'dp'))  16.2 us
    dot_general x1, matrix products, shards(): jnp.dot(exchanged, lax.all_gather(attn, ('outer', 'dp'), axis=0, tiled=Tr...  14.6 us
    psum x1, blocking collectives, shards(): lax.psum(jnp.stack([jnp.sum(z * z, axis=0), jnp.sum(z * both, axis=0)]),...  8.91 us
  transfers between devices with their start and end apart: 4, of which 2 were waited for; matrix products, arithmetic and copies ran while one was open for 2% of the time, Pallas kernels for 0%

commit v1 on v0

--- a/solution.py
+++ b/solution.py
@@ -2,6 +2,14 @@
 import jax.numpy as jnp
 from jax import lax
 from jax.sharding import PartitionSpec as P
+
+
+def trace_slots_up(s0, ndim_at):
+    s0 = jnp.moveaxis(s0, 0, ndim_at)
+    block_out = s0.shape
+    return s0.reshape(
+        *block_out[:ndim_at], block_out[ndim_at] * block_out[ndim_at + 1], *block_out[ndim_at + 2 :]
+    )
 
 
 def shards(attn, out_weight, resid, norm_gain, head, lengths, pairs, pair_valid, loss_scale):
@@ -43,7 +51,18 @@
     dproj = weight[None, :] * both - z * (inv**3 * dscore * sums[1] / width)[None, :]
     dproj = dproj.astype(jnp.bfloat16)
     zsum = jnp.sum(z * weight[None, :], axis=1)
-    gathered = lax.all_gather(dproj, "tensor", axis=0, tiled=True)
+    devs = lax.axis_size("tensor")
+    s = 0
+    leaves = []
+    while s < devs:
+        leaves.append((s, (s + 1) % devs))
+        s += 1
+    copies = [dproj]
+    while len(copies) < devs:
+        copies.append(lax.ppermute(copies[-1], axis_name="tensor", perm=leaves))
+    mid_arr = lax.axis_index("tensor")
+    copies = jnp.stack(copies, axis=0)[(mid_arr - jnp.arange(devs)) % devs]
+    gathered = trace_slots_up(copies, 0)
     exchanged = lax.all_to_all(gathered, ("outer", "dp"), split_axis=0, concat_axis=1, tiled=True)
     grad_out_proj = jnp.dot(
         exchanged,

time: 369 us -> 341 us (0.924)
  blocking collectives: 197 us -> 134 us
  waiting for transfers between devices: 98.9 us -> 125 us
  local copies, waits for them, and re-layouts: 7.01 us -> 13 us
    ppermute x0 -> x3, waiting for transfers between devices: none -> 78 us  [shards(): copies.append(lax.ppermute(copies[-1], axis_name='tensor', perm=leaves))]
    psum x1, blocking collectives: 172 us -> 104 us  [shards(): zsum, loss_sum = lax.psum((zsum, loss_part), ('outer', 'dp'))]
    all_gather x1 -> x0, waiting for transfers between devices: 50.8 us -> none  [shards(): gathered = lax.all_gather(dproj, 'tensor', axis=0, tiled=True)]
    gather x0 -> x1, local copies, waits for them, and re-layouts: none -> 4.96 us  [shards(): copies = jnp.stack(copies, axis=0)[(mid_arr - jnp.arange(devs)) % devs]]
    psum x1, blocking collectives: 16.2 us -> 20.6 us  [shards(): count = lax.psum(jnp.sum(valid), ('outer', 'dp'))]
  transfers between devices with their start and end apart: 4 -> 6, of which waited for: 2 -> 4; matrix products, arithmetic and copies ran while one was open for 2% -> 6% of each run, Pallas kernels for 0% -> 0%
where the time goes in v1:
time: 341 us
  blocking collectives  134 us (39%)
  waiting for transfers between devices  125 us (37%)
  matrix products  31.4 us (9%)
  between operations  17.3 us (5%)
  local copies, waits for them, and re-layouts  13 us (4%)
  other arithmetic  10 us (3%)
  starting transfers between devices  9.95 us (3%)
    psum x1, blocking collectives, shards(): zsum, loss_sum = lax.psum((zsum, loss_part), ('outer', 'dp'))  104 us
    ppermute x3, waiting for transfers between devices, shards(): copies.append(lax.ppermute(copies[-1], axis_name='tensor', perm=leaves))  78 us
    all_to_all x1, waiting for transfers between devices, shards(): lax.all_to_all(part, 'tensor', split_axis=0, concat_axis=0, tiled=True)  46.6 us
    psum x1, blocking collectives, shards(): count = lax.psum(jnp.sum(valid), ('outer', 'dp'))  20.6 us
    dot_general x1, matrix products, shards(): lax.dot_general(out_weight, attn, (((1,), (1,)), ((), ())), preferred_ele...  16.7 us
    dot_general x1, matrix products, shards(): jnp.dot(exchanged, lax.all_gather(attn, ('outer', 'dp'), axis=0, tiled=Tr...  14.6 us
    psum x1, blocking collectives, shards(): lax.psum(jnp.stack([jnp.sum(z * z, axis=0), jnp.sum(z * both, axis=0)]),...  8.97 us
  transfers between devices with their start and end apart: 6, of which 4 were waited for; matrix products, arithmetic and copies ran while one was open for 6% of the time, Pallas kernels for 0%

profile of v1, /device:TPU:0, one launch (start us, length us, event | category | flops | bytes accessed | tf_op | source)
XLA Modules:
  0.0 340.7 jit_solution(6954757311194164346)
XLA Ops:
  7.2 16.7 %convolution_convert_fusion = bf16[8192,256]{1,0:T(8,128)(2,1)} fusion(bf16[8192,2048]{1,0:T(8,128)(2,1)} %param.10, bf16[256,2048]{1,0:T(8,128)(2,1)} %param.9), kind=kOutput, calls=%fused_computation.1 | convolution fusion | flops 8592031744 | bytes 38797312 | tf_op jit(solution)/shard_map/dot_general | solution.py:25
  23.9 0.0 copy-start.1
  23.9 0.0 copy-start.4
  23.9 0.0 copy-start.6
  23.9 0.0 copy-start.2
  23.9 0.0 copy-start.3
  23.9 5.3 %all-to-all-start = ((bf16[4,2048,256]{2,1,0:T(8,128)(2,1)}), bf16[4,2048,256]{2,1,0:T(8,128)(2,1)}, u32[]{:S(2)}, u32[]{:S(2)}) async-start(bf16[4,2048,256]{2,1,0:T(8,128)(2,1)} %bitcast.37), calls=%async_computation | async-start | bytes 8388608 | tf_op jit(solution)/shard_map/all_to_all | solution.py:27
  29.3 0.0 all-gather.2.cloned.1.call-start
  29.3 0.7 all-gather.2.cloned.1.call-update
  30.0 0.0 copy-done.1
  30.0 0.5 copy.16
  30.6 0.0 copy-done.4
  31.2 0.0 copy-done.6
  31.3 0.0 copy-done.2
  31.3 0.0 copy-done.3
  31.3 0.0 copy-start.5
  31.3 46.6 %all-to-all-done = bf16[4,2048,256]{2,1,0:T(8,128)(2,1)} async-done(((bf16[4,2048,256]{2,1,0:T(8,128)(2,1)}), bf16[4,2048,256]{2,1,0:T(8,128)(2,1)}, u32[]{:S(2)}, u32[]{:S(2)}) %all-to-all-start) | async-done | bytes 4194336 | tf_op jit(solution)/shard_map/all_to_all | solution.py:27
  77.9 3.0 convert_reduce_fusion
  80.9 0.4 multiply_reduce_fusion.2
  81.3 9.0 %psum.28 = f32[2,256]{1,0:T(2,128)S(1)} all-reduce(f32[2,256]{1,0:T(2,128)S(1)} %pad_maximum_fusion.1), channel_id=1, replica_groups=mesh['outer'=2,'dp'=4,'tensor'=4] {'tensor'}, use_global_device_ids=true, to_apply=%region_3.0 | all-reduce | flops 512 | bytes 4096 | tf_op jit(solution)/shard_map/psum | solution.py:32
  90.3 0.2 multiply_reduce_fusion.4
  90.5 0.2 multiply_reduce_fusion.6
  90.7 0.0 copy-done.5
  90.7 0.6 convert_reduce_fusion.1
  91.3 20.6 %psum.30 = f32[]{:T(128)} all-reduce(f32[]{:T(128)} %get-tuple-element.6), channel_id=1, replica_groups=mesh['outer'=2,'dp'=4,'tensor'=4] {'outer','dp'}, use_global_device_ids=true, to_apply=%region_9.10 | all-reduce | flops 1 | bytes 8 | tf_op jit(solution)/shard_map/psum | solution.py:24
  111.9 0.7 fusion.11
  112.5 0.1 multiply_reduce_fusion.5
  112.6 0.1 multiply_reduce_fusion.3
  112.7 0.8 subtract_convert_fusion
  113.5 0.0 copy-start
  113.5 1.1 copy-done
  114.6 0.0 collective-permute-start
  114.6 26.7 %collective-permute-done = bf16[2048,256]{1,0:T(8,128)(2,1)S(1)} collective-permute-done((bf16[2048,256]{1,0:T(8,128)(2,1)S(1)}, bf16[2048,256]{1,0:T(8,128)(2,1)S(1)}, u32[]{:S(2)}, u32[]{:S(2)}) %collective-permute-start) | collective-permute-done | bytes 1048608 | tf_op jit(solution)/shard_map/ppermute | solution.py:62
  141.3 0.0 collective-permute-start.1
  141.3 26.1 %collective-permute-done.1 = bf16[2048,256]{1,0:T(8,128)(2,1)S(1)} collective-permute-done((bf16[2048,256]{1,0:T(8,128)(2,1)S(1)}, bf16[2048,256]{1,0:T(8,128)(2,1)S(1)}, u32[]{:S(2)}, u32[]{:S(2)}) %collective-permute-start.1) | collective-permute-done | bytes 1048608 | tf_op jit(solution)/shard_map/ppermute | solution.py:62
  167.4 0.0 collective-permute-start.2
  167.4 25.2 %collective-permute-done.2 = bf16[2048,256]{1,0:T(8,128)(2,1)S(1)} collective-permute-done((bf16[2048,256]{1,0:T(8,128)(2,1)S(1)}, bf16[2048,256]{1,0:T(8,128)(2,1)S(1)}, u32[]{:S(2)}, u32[]{:S(2)}) %collective-permute-start.2) | collective-permute-done | bytes 1048608 | tf_op jit(solution)/shard_map/ppermute | solution.py:62
  192.6 3.3 pad_maximum_fusion
  195.9 5.0 %gather_fusion = bf16[4,2048,256]{2,1,0:T(8,128)(2,1)} fusion(bf16[4,2048,256]{2,1,0:T(8,128)(2,1)} %pad_maximum_fusion, s32[1024]{0:T(1024)S(1)} %pad_clamp_fusion), kind=kCustom, calls=%fused_computation | custom fusion | bytes 8388624 | tf_op jit(solution)/shard_map/gather | solution.py:64
  200.9 4.6 %all-to-all-start.1 = ((bf16[8,1024,256]{2,1,0:T(8,128)(2,1)}), bf16[8,1024,256]{2,1,0:T(8,128)(2,1)}, u32[]{:S(2)}, u32[]{:S(2)}) async-start(bf16[8,1024,256]{2,1,0:T(8,128)(2,1)} %bitcast.36), calls=%async_computation.1 | async-start | bytes 8388608 | tf_op jit(solution)/shard_map/all_to_all | solution.py:66
  205.5 104.2 %all-reduce = (f32[]{:T(128)}, f32[2048]{0:T(1024)S(1)}) all-reduce(f32[]{:T(128)} %get-tuple-element.7, f32[2048]{0:T(1024)S(1)} %get-tuple-element.11), channel_id=1, replica_groups=mesh['outer'=2,'dp'=4,'tensor'=4] {'outer','dp'}, use_global_device_ids=true, to_apply=%region_7.8 | all-reduce | flops 2049 | bytes 16392 | tf_op jit(solution)/shard_map/psum | solution.py:72
  311.0 0.6 convert_multiply_fusion
  311.6 0.0 all-to-all-done.1
  311.6 6.5 %copy.17 = bf16[1024,8,256]{0,2,1:T(8,128)(2,1)} copy(bf16[1024,8,256]{2,0,1:T(8,128)(2,1)} %bitcast.18) | data formatting | bytes 8388608 | tf_op jit(solution)/shard_map/all_to_all | solution.py:66
  318.1 0.0 all-gather.2.cloned.1.call-done
  318.1 14.6 %fusion.13 = f32[1024,2048]{1,0:T(8,128)} fusion(bf16[1024,2048]{0,1:T(8,128)(2,1)} %bitcast.38, bf16[2048,2048]{1,0:T(8,128)(2,1)} %all-gather.2.cloned.1.call-done), kind=kOutput, calls=%fused_computation.53 | convolution fusion | flops 8589934592 | bytes 20971520 | tf_op jit(solution)/shard_map/dot_general | solution.py:67
  (9 shorter events, 0.1 us)
Async XLA Ops:
  23.9 6.1 %copy-start.1 = (bf16[256,2048]{1,0:T(8,128)(2,1)S(1)}, bf16[256,2048]{1,0:T(8,128)(2,1)}, u32[]{:S(2)}) copy-start(bf16[256,2048]{1,0:T(8,128)(2,1)} %param.11) | copy-start | bytes 3145732
  23.9 6.6 %copy-start.4 = (s32[4]{0:T(128)S(1)}, s32[4]{0:T(128)}, u32[]{:S(2)}) copy-start(s32[4]{0:T(128)} %param.14) | copy-start | bytes 52
  23.9 7.3 %copy-start.6 = (s32[4,2]{0,1:T(2,128)S(1)}, s32[4,2]{0,1:T(2,128)}, u32[]{:S(2)}) copy-start(s32[4,2]{0,1:T(2,128)} %param.15) | copy-start | bytes 100
  23.9 7.3 %copy-start.2 = (bf16[2048]{0:T(1024)(128)(2,1)S(1)}, bf16[2048]{0:T(1024)(128)(2,1)}, u32[]{:S(2)}) copy-start(bf16[2048]{0:T(1024)(128)(2,1)} %param.12) | copy-start | bytes 12292
  23.9 7.3 %copy-start.3 = (bf16[2048]{0:T(1024)(128)(2,1)S(1)}, bf16[2048]{0:T(1024)(128)(2,1)}, u32[]{:S(2)}) copy-start(bf16[2048]{0:T(1024)(128)(2,1)} %param.13) | copy-start | bytes 12292
  23.9 53.9 %all-to-all-start = ((bf16[4,2048,256]{2,1,0:T(8,128)(2,1)}), bf16[4,2048,256]{2,1,0:T(8,128)(2,1)}, u32[]{:S(2)}, u32[]{:S(2)}) async-start(bf16[4,2048,256]{2,1,0:T(8,128)(2,1)} %bitcast.37), calls=%async_computation | async-start | bytes 8388608 | tf_op jit(solution)/shard_map/all_to_all | solution.py:27
  29.3 288.8 %all-gather.2.cloned.1.call-start = ((), (), s32[]{:S(2)}) async-start(), calls=%async_computation.2 | async-start | bytes 9437184 | tf_op jit(solution)/shard_map/all_gather | solution.py:69
  31.3 59.4 %copy-start.5 = (s32[4]{0:T(128)S(1)}, s32[4]{0:T(128)}, u32[]{:S(2)}) copy-start(s32[4]{0:T(128)} %param.16) | copy-start | bytes 52
  113.5 1.1 copy-start
  114.6 26.7 %collective-permute-start = (bf16[2048,256]{1,0:T(8,128)(2,1)S(1)}, bf16[2048,256]{1,0:T(8,128)(2,1)S(1)}, u32[]{:S(2)}, u32[]{:S(2)}) collective-permute-start(bf16[2048,256]{1,0:T(8,128)(2,1)S(1)} %get-tuple-element.10), channel_id=1, source_target_pairs={{0,1},{1,2},{2,3},{3,0},{4,5},{5,6},{6,7},{7,4},{8,9},{9,10},{10,1... | collective-permute-start | bytes 3145736 | tf_op jit(solution)/shard_map/ppermute | solution.py:62
  141.3 26.1 %collective-permute-start.1 = (bf16[2048,256]{1,0:T(8,128)(2,1)S(1)}, bf16[2048,256]{1,0:T(8,128)(2,1)S(1)}, u32[]{:S(2)}, u32[]{:S(2)}) collective-permute-start(bf16[2048,256]{1,0:T(8,128)(2,1)S(1)} %collective-permute-done), channel_id=1, source_target_pairs={{0,1},{1,2},{2,3},{3,0},{4,5},{5,6},{6,7},{7,4},{8,9},{9,10},{10,1... | collective-permute-start | bytes 3145736 | tf_op jit(solution)/shard_map/ppermute | solution.py:62
  167.4 25.2 %collective-permute-start.2 = (bf16[2048,256]{1,0:T(8,128)(2,1)S(1)}, bf16[2048,256]{1,0:T(8,128)(2,1)S(1)}, u32[]{:S(2)}, u32[]{:S(2)}) collective-permute-start(bf16[2048,256]{1,0:T(8,128)(2,1)S(1)} %collective-permute-done.1), channel_id=1, source_target_pairs={{0,1},{1,2},{2,3},{3,0},{4,5},{5,6},{6,7},{7,4},{8,9},{9,10},{10,1... | collective-permute-start | bytes 3145736 | tf_op jit(solution)/shard_map/ppermute | solution.py:62
  200.9 110.7 %all-to-all-start.1 = ((bf16[8,1024,256]{2,1,0:T(8,128)(2,1)}), bf16[8,1024,256]{2,1,0:T(8,128)(2,1)}, u32[]{:S(2)}, u32[]{:S(2)}) async-start(bf16[8,1024,256]{2,1,0:T(8,128)(2,1)} %bitcast.36), calls=%async_computation.1 | async-start | bytes 8388608 | tf_op jit(solution)/shard_map/all_to_all | solution.py:66
Sparse Core Ops, SparseCore 0:
  31.7 85.4 all-gather.1
